TPU v7x, 32 devices: a whole 2x2x4 slice. The times are simulated.
32 devices in a mesh: seq: 8 (over z, x), wsh: 4 (over y, core).
Axes of the slice: x: 2, y: 2, z: 4, core: 2. Of those that a mesh axis runs over, the one named last changes fastest.
Arguments:
- tokens_in: bfloat16 [4, 4096, 1024], P('wsh', 'seq'), may hold values from -6 to 6
- out_grad: bfloat16 [4, 4096, 1024], P('wsh', 'seq'), may hold values from -6 to 6
- deal_order: int32 [8], replicated, may hold values from 0 to 7, each once
- seq_lengths: int32 [4, 4], P('wsh'), may hold values from 1 to 2048, 4096 in all within a row
- weights: bfloat16 [1024, 17920], P('wsh'), may hold values from -0.1875 to 0.1875
- norm_gains: bfloat16 [2, 1024], P(None, 'wsh'), may hold values from 0.5 to 1.5
- conv_kernel: bfloat16 [3, 1024], P(None, 'wsh'), may hold values from -3 to 3
- vector_state: float32 [5, 1024], P(None, 'wsh'), may hold values from 0.2 to 5
- kron_stats: float32 [2, 1120, 128, 128], P(None, 'wsh', 'seq'), may hold values from -6 to 6
- kron_roots: float32 [2, 1120, 128, 128], P(None, 'wsh', 'seq'), as said below
Outputs:
- block_out: bfloat16 [4, 4096, 1024], P('wsh', 'seq')
- input_grad: bfloat16 [4, 4096, 1024], P('wsh', 'seq')
- weight_grad: float32 [1024, 17920], P('wsh')
- vector_grad: float32 [5, 1024], P(None, 'wsh')
- vector_state_new: float32 [5, 1024], P(None, 'wsh')
- vector_update: float32 [5, 1024], P(None, 'wsh')
- kron_stats_new: float32 [2, 1120, 128, 128], P(None, 'wsh', 'seq')
- weight_update: float32 [1120, 128, 128], P('wsh', 'seq')
Inputs may be any that keep to these rules, and one draw needn't show every extreme that they name: `deal_order`: a permutation of 0 to 7. `seq_lengths`: each row sums to 4096; in every pack the longest sequence has exactly 2048 tokens. `kron_roots`: each block has a dominant diagonal between 0.5 and 2.
All inputs are finite; a program needn't handle non-finite values.
Results may differ from a plain program's by a relative error of at most 0.025.
Values may be sent and summed in bfloat16 or wider, within the bound.
A program may use at most 320 MiB of HBM per device.

v0:
```python
import jax
import jax.numpy as jnp
from jax import lax
from jax.sharding import PartitionSpec as P

D = 1024
FF = 4608
BLK = 128
EPS = 1e-05
BETA = 0.5
BETA_VEC = 0.5
LEARN = 0.03
LEARN_VEC = 0.05
HIGH = lax.Precision.HIGHEST


def passed_along(block, axis, distance):
    devices = range(lax.axis_size(axis))
    route = [(i - distance, i) for i in devices if i - distance in devices]
    return lax.ppermute(block, axis, route)


def seq_positions(lengths_row, first, count):
    starts = jnp.cumsum(lengths_row) - lengths_row
    rows_at = first + jnp.arange(count, dtype=jnp.int32)
    begin = jnp.max(jnp.where(starts[None, :] <= rows_at[:, None], starts[None, :], 0), axis=1)
    return rows_at - begin


def rms_scale(values):
    return lax.rsqrt(jnp.mean(values * values, axis=1, keepdims=True) + EPS)


def norm_back(upstream, values, scale, gain):
    scaled = upstream * gain
    inner = jnp.mean(scaled * values, axis=1, keepdims=True)
    return (
        scale * scaled - values * scale * scale * scale * inner,
        jnp.sum(upstream * values * scale, axis=0),
    )


def contract_rows(left, right):
    return lax.dot_general(
        left, right, (((0,), (0,)), ((), ())), preferred_element_type=jnp.float32
    )


def contract_cols(left, right):
    return lax.dot_general(
        left, right, (((1,), (1,)), ((), ())), preferred_element_type=jnp.float32
    )


def shards(
    tokens_in,
    out_grad,
    deal_order,
    seq_lengths,
    weights,
    norm_gains,
    conv_kernel,
    vector_state,
    kron_stats,
    kron_roots,
):
    n_seq = lax.axis_size("seq")
    n_wsh = lax.axis_size("wsh")
    rows = tokens_in.shape[1]
    unit = rows // n_seq
    arrived = (
        lax.all_to_all(
            tokens_in.reshape(n_seq, unit, D), "seq", split_axis=0, concat_axis=0, tiled=True
        ),
        lax.all_to_all(
            out_grad.reshape(n_seq, unit, D), "seq", split_axis=0, concat_axis=0, tiled=True
        ),
    )
    x_bf = jnp.take(arrived[0], deal_order, axis=0).reshape(rows, D)
    dy_bf = jnp.take(arrived[1], deal_order, axis=0).reshape(rows, D)
    full_w, gains_bf, kernel_bf = (
        lax.all_gather(weights, "wsh", axis=0, tiled=True),
        lax.all_gather(norm_gains, "wsh", axis=1, tiled=True),
        lax.all_gather(conv_kernel, "wsh", axis=1, tiled=True),
    )
    gains = gains_bf.astype(jnp.float32)
    kernel = kernel_bf.astype(jnp.float32)
    first_row = lax.axis_index("seq") * rows
    pos = seq_positions(seq_lengths[0], first_row, rows + 2)
    masks = [(pos >= 2 - k).astype(jnp.float32)[:, None] for k in range(3)]
    xf = x_bf.astype(jnp.float32)
    scale_one = rms_scale(xf)
    xn = (xf * scale_one * gains[0]).astype(jnp.bfloat16)
    proj = jnp.dot(xn, full_w[:, : 3 * D], preferred_element_type=jnp.float32)
    b_part = proj[:, :D]
    c_part = proj[:, D : 2 * D]
    x_part = proj[:, 2 * D :]
    conv_in = b_part * x_part
    prev = passed_along(conv_in[rows - 2 :], "seq", 1)
    ext = jnp.concatenate([prev, conv_in], axis=0)
    conv = (
        kernel[0] * masks[0][:rows] * ext[0:rows]
        + kernel[1] * masks[1][:rows] * ext[1 : rows + 1]
        + kernel[2] * masks[2][:rows] * ext[2 : rows + 2]
    )
    yc = (c_part * conv).astype(jnp.bfloat16)
    hidden_sum = xf + jnp.dot(yc, full_w[:, 3 * D : 4 * D], preferred_element_type=jnp.float32)
    scale_two = rms_scale(hidden_sum)
    hn = (hidden_sum * scale_two * gains[1]).astype(jnp.bfloat16)
    gate_up = jnp.dot(hn, full_w[:, 4 * D : 4 * D + 2 * FF], preferred_element_type=jnp.float32)
    gate = gate_up[:, :FF]
    upper = gate_up[:, FF:]
    sig = jax.nn.sigmoid(gate)
    act = (gate * sig * upper).astype(jnp.bfloat16)
    ffn = contract_cols(act, full_w[:, 4 * D + 2 * FF :])
    result = (hidden_sum + ffn).astype(jnp.bfloat16)
    g_down = contract_rows(dy_bf, act)
    d_act = jnp.dot(dy_bf, full_w[:, 4 * D + 2 * FF :], preferred_element_type=jnp.float32)
    d_gate = d_act * upper * sig * (1.0 + gate * (1.0 - sig))
    d_upper = d_act * gate * sig
    d_gu = jnp.concatenate([d_gate, d_upper], axis=1).astype(jnp.bfloat16)
    g_gu = contract_rows(hn, d_gu)
    d_hn = contract_cols(d_gu, full_w[:, 4 * D : 4 * D + 2 * FF])
    d_norm_two, g_gain_two = norm_back(d_hn, hidden_sum, scale_two, gains[1])
    d_hidden = dy_bf.astype(jnp.float32) + d_norm_two
    d_mix = d_hidden.astype(jnp.bfloat16)
    g_out = contract_rows(yc, d_mix)
    d_yc = contract_cols(d_mix, full_w[:, 3 * D : 4 * D])
    d_c = d_yc * conv
    d_conv = d_yc * c_part
    after = passed_along(d_conv[:2], "seq", -1)
    d_ext = jnp.concatenate([d_conv, after], axis=0)
    weighted = [d_ext * masks[k] for k in range(3)]
    d_bx = (
        kernel[2] * weighted[2][:rows]
        + kernel[1] * weighted[1][1 : rows + 1]
        + kernel[0] * weighted[0][2 : rows + 2]
    )
    g_taps = jnp.stack([jnp.sum(weighted[k][:rows] * ext[k : k + rows], axis=0) for k in range(3)])
    d_proj = jnp.concatenate([d_bx * x_part, d_c, d_bx * b_part], axis=1).astype(jnp.bfloat16)
    g_in = contract_rows(xn, d_proj)
    d_xn = contract_cols(d_proj, full_w[:, : 3 * D])
    d_norm_one, g_gain_one = norm_back(d_xn, xf, scale_one, gains[0])
    d_input = (d_hidden + d_norm_one).astype(jnp.bfloat16)
    g_vec = jnp.concatenate([g_gain_one[None], g_gain_two[None], g_taps], axis=0)
    inverse = jnp.argsort(deal_order)
    leaving = (
        jnp.take(result.reshape(n_seq, unit, D), inverse, axis=0),
        jnp.take(d_input.reshape(n_seq, unit, D), inverse, axis=0),
    )
    returned = (
        lax.all_to_all(leaving[0], "seq", split_axis=0, concat_axis=0, tiled=True),
        lax.all_to_all(leaving[1], "seq", split_axis=0, concat_axis=0, tiled=True),
    )
    summed = (
        lax.psum_scatter(g_in.astype(jnp.bfloat16), "wsh", scatter_dimension=0, tiled=True).astype(
            jnp.float32
        ),
        lax.psum_scatter(g_out.astype(jnp.bfloat16), "wsh", scatter_dimension=0, tiled=True).astype(
            jnp.float32
        ),
        lax.psum_scatter(g_gu.astype(jnp.bfloat16), "wsh", scatter_dimension=0, tiled=True).astype(
            jnp.float32
        ),
        lax.psum_scatter(
            g_down.astype(jnp.bfloat16), "wsh", scatter_dimension=0, tiled=True
        ).astype(jnp.float32),
        lax.psum_scatter(g_vec.astype(jnp.bfloat16), "wsh", scatter_dimension=1, tiled=True).astype(
            jnp.float32
        ),
    )
    summed = (
        lax.psum(summed[0].astype(jnp.bfloat16), "seq").astype(jnp.float32),
        lax.psum(summed[1].astype(jnp.bfloat16), "seq").astype(jnp.float32),
        lax.psum(summed[2].astype(jnp.bfloat16), "seq").astype(jnp.float32),
        lax.psum(summed[3].astype(jnp.bfloat16), "seq").astype(jnp.float32),
        lax.psum(summed[4].astype(jnp.bfloat16), "seq").astype(jnp.float32),
    )
    grad_scale = lax.rsqrt(jnp.asarray(rows * n_seq * n_wsh, jnp.float32))
    grad_shard = jnp.concatenate([summed[0], summed[1], summed[2], summed[3]], axis=1) * grad_scale
    vec_grad = summed[4] * grad_scale
    state_new = BETA_VEC * vector_state + (1.0 - BETA_VEC) * vec_grad * vec_grad
    vec_update = -LEARN_VEC * vec_grad * lax.rsqrt(state_new)
    nrow_blocks = grad_shard.shape[0] // BLK
    ncol_blocks = grad_shard.shape[1] // BLK
    grad_blocks = (
        grad_shard.reshape(nrow_blocks, BLK, ncol_blocks, BLK)
        .transpose(0, 2, 1, 3)
        .reshape(nrow_blocks * ncol_blocks, BLK, BLK)
    )
    share = BLK // n_seq
    first_block_row = lax.axis_index("seq") * share
    block_rows = lax.dynamic_slice_in_dim(grad_blocks, first_block_row, share, 1)
    block_cols = lax.dynamic_slice_in_dim(grad_blocks, first_block_row, share, 2)
    left_term = jnp.einsum("nij,nkj->nik", block_rows, grad_blocks, precision=HIGH)
    right_term = jnp.einsum("nji,njk->nik", block_cols, grad_blocks, precision=HIGH)
    stats_new = jnp.stack(
        [
            BETA * kron_stats[0] + (1.0 - BETA) * left_term / BLK,
            BETA * kron_stats[1] + (1.0 - BETA) * right_term / BLK,
        ]
    )
    right_full = lax.all_gather(
        kron_roots[1].astype(jnp.bfloat16), "seq", axis=1, tiled=True
    ).astype(jnp.float32)
    left_mul = jnp.einsum("nij,njk->nik", kron_roots[0], grad_blocks, precision=HIGH)
    update = -LEARN * jnp.einsum("nij,njk->nik", left_mul, right_full, precision=HIGH)
    return (
        returned[0].reshape(1, rows, D),
        returned[1].reshape(1, rows, D),
        grad_shard,
        vec_grad,
        state_new,
        vec_update,
        stats_new,
        update,
    )


def solution(mesh):
    return jax.shard_map(
        shards,
        mesh=mesh,
        in_specs=(
            P("wsh", "seq", None),
            P("wsh", "seq", None),
            P(),
            P("wsh", None),
            P("wsh", None),
            P(None, "wsh"),
            P(None, "wsh"),
            P(None, "wsh"),
            P(None, "wsh", "seq", None),
            P(None, "wsh", "seq", None),
        ),
        out_specs=(
            P("wsh", "seq", None),
            P("wsh", "seq", None),
            P("wsh", None),
            P(None, "wsh"),
            P(None, "wsh"),
            P(None, "wsh"),
            P(None, "wsh", "seq", None),
            P("wsh", "seq", None),
        ),
        check_vma=False,
    )
```

profile of v0, /device:TPU:0, one launch (start us, length us, event | category | flops | bytes accessed | tf_op | source)
XLA Modules:
  0.0 1136.9 jit_solution(3107054169689322003)
XLA Ops:
  15.6 25.6 %all-to-all-done = bf16[8,64,1024]{2,1,0:T(8,128)(2,1)S(1)} async-done(((bf16[8,64,1024]{2,1,0:T(8,128)(2,1)}), bf16[8,64,1024]{2,1,0:T(8,128)(2,1)S(1)}, u32[]{:S(2)}, u32[]{:S(2)}) %all-to-all-start) | async-done | bytes 1048608 | tf_op jit(solution)/shard_map/all_to_all | solution.py:72
  57.4 13.6 %all-to-all-done.2 = bf16[8,64,1024]{2,1,0:T(8,128)(2,1)} async-done(((bf16[8,64,1024]{2,1,0:T(8,128)(2,1)}), bf16[8,64,1024]{2,1,0:T(8,128)(2,1)}, u32[]{:S(2)}, u32[]{:S(2)}) %all-to-all-start.2) | async-done | bytes 1048608 | tf_op jit(solution)/shard_map/all_to_all | solution.py:75
  74.1 159.7 %all-gather.4.cloned.1.call-done = bf16[1024,17920]{1,0:T(8,128)(2,1)} async-done(((bf16[256,17920]{1,0:T(8,128)(2,1)}), bf16[1024,17920]{1,0:T(8,128)(2,1)}) %all-gather.4.cloned.1.call-update) | async-done | bytes 36700176 | tf_op jit(solution)/shard_map/all_gather | solution.py:82
  250.3 18.3 %fusion.4 = f32[512,9216]{1,0:T(8,128)} fusion(bf16[1024,17920]{1,0:T(8,128)(2,1)} %all-gather.4.cloned.1.call-done, f32[512,1024]{1,0:T(8,128)S(1)} %get-tuple-element.51, f32[1024]{0:T(1024)S(1)} %bitcast.99, f32[512]{0:T(512)S(1)} %add_rsqrt_fusion.1), kind=kOutput, calls=%fused_computation.10 | convolution fusion | flops 9665249280 | bytes 39852032 | tf_op jit(solution)/shard_map/dot_general | solution.py:110
  268.6 17.8 %multiply_convert_fusion.1 = (bf16[512,4608]{1,0:T(8,128)(2,1)}, bf16[512,4608]{1,0:T(8,128)(2,1)}, bf16[512,4608]{1,0:T(8,128)(2,1)}) fusion(f32[512,9216]{1,0:T(8,128)} %fusion.4, bf16[512,1024]{1,0:T(8,128)(2,1)} %bitcast.86, bf16[1024,17920]{1,0:T(8,128)(2,1)} %all-gather.4.cloned.1.call-done), kind=kOutput, calls=%fused_computation.15 | convolution fusion | flops 4869586944 | bytes 43515904 | tf_op jit(solution)/shard_map/dot_general | solution.py:118
  286.4 16.0 %multiply_reduce_fusion.1 = (bf16[1024]{0:T(1024)(128)(2,1)S(1)}, f32[512]{0:T(512)S(1)}, f32[512,1024]{1,0:T(8,128)S(1)}) fusion(f32[512,1024]{1,0:T(8,128)} %copy-done.10, f32[512]{0:T(512)S(1)} %add_rsqrt_fusion.1, f32[1024]{0:T(1024)S(1)} %bitcast.100, bf16[1024,17920]{1,0:T(8,128)(2,1)} %all-gather.4.cloned.1.call-done, ...), kind=kOutput, calls=%fused_computation.75 | convolution fusion | flops 9685694464 | bytes 32516096 | tf_op jit(solution)/shard_map/dot_general | solution.py:50
  331.1 9.8 convolution_convert_fusion.1
  342.6 17.8 %convolution_convert_fusion = bf16[1024,9216]{1,0:T(8,128)(2,1)} fusion(bf16[512,4608]{1,0:T(8,128)(2,1)} %get-tuple-element.32, bf16[512,4608]{1,0:T(8,128)(2,1)} %get-tuple-element.31, f32[512,1024]{1,0:T(8,128)S(1)} %copy-done.12, f32[1024]{0:T(1024)S(1)} %bitcast.102, f32[512]{0:T(512)S(1)} %add_rsqrt_fusion.1), kind=kOutput, calls=%fused_computation.7 | convolution fusion | flops 9693560832 | bytes 30414848 | tf_op jit(solution)/shard_map/dot_general | solution.py:44
  360.4 9.6 fusion.41
  370.8 30.0 %reduce-scatter.6.cloned.1.call-done = bf16[256,3072]{1,0:T(8,128)(2,1)} async-done(((bf16[1024,3072]{1,0:T(8,128)(2,1)}), bf16[256,3072]{1,0:T(8,128)(2,1)}) %reduce-scatter.6.cloned.1.call-update) | async-done | bytes 1572880 | tf_op jit(solution)/shard_map/reduce_scatter | solution.py:156
  400.9 81.0 %reduce-scatter.12.cloned.1.call-done = bf16[256,4608]{1,0:T(8,128)(2,1)} async-done(((bf16[1024,4608]{1,0:T(8,128)(2,1)}), bf16[256,4608]{1,0:T(8,128)(2,1)}) %reduce-scatter.12.cloned.1.call-update) | async-done | bytes 2359312 | tf_op jit(solution)/shard_map/reduce_scatter | solution.py:165
  481.9 140.3 %reduce-scatter.10.cloned.1.call-done = bf16[256,9216]{1,0:T(8,128)(2,1)} async-done(((bf16[1024,9216]{1,0:T(8,128)(2,1)}), bf16[256,9216]{1,0:T(8,128)(2,1)}) %reduce-scatter.10.cloned.1.call-update) | async-done | bytes 4718608 | tf_op jit(solution)/shard_map/reduce_scatter | solution.py:162
  626.1 9.9 add_convert_fusion
  645.4 58.2 %all_to_all.20 = bf16[8,64,1024]{2,1,0:T(8,128)(2,1)S(1)} all-to-all(bf16[8,64,1024]{2,1,0:T(8,128)(2,1)S(1)} %get-tuple-element.49), channel_id=1, replica_groups=mesh['seq'=8,'wsh'=4] {'seq'}, dimensions={0} | all-to-all | bytes 2097152 | tf_op jit(solution)/shard_map/all_to_all | solution.py:152
  707.3 49.4 %psum.39 = bf16[5,256]{1,0:T(8,128)(2,1)S(1)} all-reduce(bf16[5,256]{1,0:T(8,128)(2,1)} %reduce-scatter.14.cloned.1.call-done), channel_id=1, replica_groups=mesh['seq'=8,'wsh'=4] {'seq'}, use_global_device_ids=true, to_apply=%region_21.23 | all-reduce | flops 1280 | bytes 5120 | tf_op jit(solution)/shard_map/psum | solution.py:177
  758.3 222.7 %all-reduce.3.cloned.1.call-done = (bf16[256,4608]{1,0:T(8,128)(2,1)}, bf16[256,9216]{1,0:T(8,128)(2,1)}, bf16[256,1024]{1,0:T(8,128)(2,1)}, bf16[256,3072]{1,0:T(8,128)(2,1)}) async-done(((bf16[256,4608]{1,0:T(8,128)(2,1)}, bf16[256,9216]{1,0:T(8,128)(2,1)}, bf16[256,1024]{1,0:T(8,128)(2,1)}, bf16[256,3072]{1,0:T(8,128)(2,1)}), (bf16[256,4608]{1,0:T(8,128)(2,1)}, bf16[256,9216]{1,0:T(8,128)(2,1)}, ...) | async-done | bytes 9175056 | tf_op jit(solution)/shard_map/psum | solution.py:176
  980.9 10.2 convert_multiply_fusion
  991.1 19.2 %mul.433 = f32[2,128,140,128]{3,2,1,0:T(8,128)} reshape(f32[256,17920]{1,0:T(8,128)} %convert_multiply_fusion) | data formatting | bytes 36700160 | tf_op jit(solution)/shard_map/mul | solution.py:180
  1010.3 12.0 %copy.22 = f32[2,140,128,128]{3,2,1,0:T(8,128)S(1)} copy(f32[2,140,128,128]{3,1,2,0:T(8,128)} %bitcast.79) | data formatting | bytes 36700160 | tf_op jit(solution)/shard_map/transpose | solution.py:188
  1022.4 29.2 %fusion.19 = f32[1,280,16,128]{3,2,1,0:T(8,128)S(1)} fusion(f32[2,280,16,128]{3,2,1,0:T(8,128)S(1)} %bitcast.83, f32[280,128,128]{2,1,0:T(8,128)S(1)} %bitcast.76, s32[]{:T(128)S(6)} %select_n.16), kind=kOutput, calls=%fused_computation.39 | convolution fusion | flops 882524160 | bytes 25231364 | tf_op jit(solution)/shard_map/nij,nkj->nik/dot_general | solution.py:195
  1051.6 35.4 %fusion.18 = f32[1,280,16,128]{3,2,1,0:T(8,128)S(1)} fusion(f32[2,280,16,128]{3,2,1,0:T(8,128)S(1)} %bitcast.83, f32[280,128,128]{2,1,0:T(8,128)S(1)} %bitcast.77, s32[]{:T(128)S(6)} %select_n.16), kind=kOutput, calls=%fused_computation.37 | convolution fusion | flops 882524160 | bytes 41287684 | tf_op jit(solution)/shard_map/nji,njk->nik/dot_general | solution.py:196
  1089.5 17.0 %fusion.16 = f32[280,128,16]{1,2,0:T(8,128)S(1)} fusion(f32[280,128,128]{2,1,0:T(8,128)S(1)} %bitcast.78, f32[2,280,16,128]{3,2,1,0:T(8,128)} %param.21), kind=kOutput, calls=%fused_computation.34 | convolution fusion | flops 880803840 | bytes 22937600 | tf_op jit(solution)/shard_map/nij,njk->nik/dot_general | solution.py:206
  1106.5 10.2 all-gather.6.cloned.1.call-done
  1116.6 10.6 fusion.54
  (145 shorter events, 98.6 us)
Async XLA Ops:
  7.2 226.6 %all-gather.4.cloned.1.call-start = ((), (), s32[]{:S(2)}) async-start(), calls=%async_computation.9 | async-start | bytes 45875200 | tf_op jit(solution)/shard_map/all_gather | solution.py:82
  7.9 37.7 %copy-start.22 = (bf16[2,256]{1,0:T(2,128)(2,1)S(1)}, bf16[2,256]{1,0:T(2,128)(2,1)}, u32[]{:S(2)}) copy-start(bf16[2,256]{1,0:T(2,128)(2,1)} %param.17) | copy-start | bytes 3076
  7.9 42.9 %copy-start.21 = (bf16[3,256]{1,0:T(4,128)(2,1)S(1)}, bf16[3,256]{1,0:T(4,128)(2,1)}, u32[]{:S(2)}) copy-start(bf16[3,256]{1,0:T(4,128)(2,1)} %param.18) | copy-start | bytes 4612
  7.9 48.2 %copy-start.24 = (s32[8]{0:T(128)S(1)}, s32[8]{0:T(128)}, u32[]{:S(2)}) copy-start(s32[8]{0:T(128)} %param.14) | copy-start | bytes 100
  7.9 33.2 %all-to-all-start = ((bf16[8,64,1024]{2,1,0:T(8,128)(2,1)}), bf16[8,64,1024]{2,1,0:T(8,128)(2,1)S(1)}, u32[]{:S(2)}, u32[]{:S(2)}) async-start(bf16[8,64,1024]{2,1,0:T(8,128)(2,1)} %bitcast), calls=%async_computation | async-start | bytes 2097152 | tf_op jit(solution)/shard_map/all_to_all | solution.py:72
  41.1 29.8 %all-to-all-start.2 = ((bf16[8,64,1024]{2,1,0:T(8,128)(2,1)}), bf16[8,64,1024]{2,1,0:T(8,128)(2,1)}, u32[]{:S(2)}, u32[]{:S(2)}) async-start(bf16[8,64,1024]{2,1,0:T(8,128)(2,1)} %bitcast.10), calls=%async_computation.2 | async-start | bytes 2097152 | tf_op jit(solution)/shard_map/all_to_all | solution.py:75
  45.4 325.4 %reduce-scatter.8.cloned.1.call-start = ((), (), s32[]{:S(2)}) async-start(), calls=%async_computation.11 | async-start | bytes 2621440 | tf_op jit(solution)/shard_map/reduce_scatter | solution.py:159
  74.1 159.7 %copy-start.18 = (bf16[512,1024]{1,0:T(8,128)(2,1)}, bf16[512,1024]{1,0:T(8,128)(2,1)S(1)}, u32[]{:S(2)}) copy-start(bf16[512,1024]{1,0:T(8,128)(2,1)S(1)} %fusion.32) | copy-start | bytes 3145732
  239.8 4.9 collective-permute-start
  250.3 18.3 %copy-start.10 = (f32[512,1024]{1,0:T(8,128)}, f32[512,1024]{1,0:T(8,128)S(1)}, u32[]{:S(2)}) copy-start(f32[512,1024]{1,0:T(8,128)S(1)} %get-tuple-element.51) | copy-start | bytes 6291460
  286.4 16.0 %copy-start.8 = (bf16[8,64,1024]{2,1,0:T(8,128)(2,1)S(1)}, bf16[8,64,1024]{2,1,0:T(8,128)(2,1)}, u32[]{:S(2)}) copy-start(bf16[8,64,1024]{2,1,0:T(8,128)(2,1)} %broadcast_select_fusion.2) | copy-start | bytes 3145732
  286.4 16.0 %copy-start.11 = (f32[512,1024]{1,0:T(8,128)S(1)}, f32[512,1024]{1,0:T(8,128)}, u32[]{:S(2)}) copy-start(f32[512,1024]{1,0:T(8,128)} %copy-done.10) | copy-start | bytes 6291460
  307.3 93.6 %reduce-scatter.6.cloned.1.call-start = ((), (), s32[]{:S(2)}) async-start(), calls=%async_computation.10 | async-start | bytes 7864320 | tf_op jit(solution)/shard_map/reduce_scatter | solution.py:156
  307.4 12.3 %slice-start = ((s8[6291456]{0:T(1024)(128)(4,1)}), s8[4194304]{0:T(1024)(128)(4,1)S(1)}, s32[]{:S(2)}) async-start(s8[6291456]{0:T(1024)(128)(4,1)} %bitcast.80), calls=%async_computation.17 | async-start | bytes 8388608
  313.5 5.8 collective-permute-start.1
  329.9 151.9 %reduce-scatter.12.cloned.1.call-start = ((), (), s32[]{:S(2)}) async-start(), calls=%async_computation.13 | async-start | bytes 11796480 | tf_op jit(solution)/shard_map/reduce_scatter | solution.py:165
  341.0 281.2 %reduce-scatter.10.cloned.1.call-start = ((), (), s32[]{:S(2)}) async-start(), calls=%async_computation.12 | async-start | bytes 23592960 | tf_op jit(solution)/shard_map/reduce_scatter | solution.py:162
  360.4 346.9 %reduce-scatter.14.cloned.1.call-start = ((), (), s32[]{:S(2)}) async-start(), calls=%async_computation.14 | async-start | bytes 20480 | tf_op jit(solution)/shard_map/reduce_scatter | solution.py:168
  370.7 610.2 %all-reduce.3.cloned.1.call-start = ((), (), s32[]{:S(2)}) async-start(), calls=%async_computation.16 | async-start | bytes 18350080 | tf_op jit(solution)/shard_map/psum | solution.py:176
  622.2 494.4 %all-gather.6.cloned.1.call-start = ((), (), s32[]{:S(2)}) async-start(), calls=%async_computation.15 | async-start | bytes 10321920 | tf_op jit(solution)/shard_map/all_gather | solution.py:203
  645.4 111.4 %copy-start.20 = (f32[5,256]{1,0:T(8,128)S(1)}, f32[5,256]{1,0:T(8,128)}, u32[]{:S(2)}) copy-start(f32[5,256]{1,0:T(8,128)} %param.19) | copy-start | bytes 15364
  703.6 54.7 %all-to-all-start.3 = ((bf16[8,64,1024]{2,1,0:T(8,128)(2,1)}), bf16[8,64,1024]{2,1,0:T(8,128)(2,1)S(1)}, u32[]{:S(2)}, u32[]{:S(2)}) async-start(bf16[8,64,1024]{2,1,0:T(8,128)(2,1)} %get-tuple-element.48), calls=%async_computation.3 | async-start | bytes 2097152 | tf_op jit(solution)/shard_map/all_to_all | solution.py:153
  758.3 222.7 %copy-start.6 = (bf16[8,64,1024]{2,1,0:T(8,128)(2,1)}, bf16[8,64,1024]{2,1,0:T(8,128)(2,1)S(1)}, u32[]{:S(2)}) copy-start(bf16[8,64,1024]{2,1,0:T(8,128)(2,1)S(1)} %all-to-all-done.3) | copy-start | bytes 3145732
  991.1 31.2 %slice-start.2 = ((s8[4587520]{0:T(1024)(128)(4,1)}), s8[393216]{0:T(1024)(128)(4,1)S(1)}, s32[]{:S(2)}) async-start(s8[4587520]{0:T(1024)(128)(4,1)} %bitcast.82), calls=%async_computation.19 | async-start | bytes 786432
  (18 other events, 71.8 us)
Sparse Core Ops, SparseCore 0:
  9.6 224.1 all-gather.3
  307.4 31.9 reduce-scatter.7
  342.0 58.8 reduce-scatter.5
  403.9 77.9 reduce-scatter.11
  484.3 137.8 reduce-scatter.9
  625.0 19.4 reduce-scatter.13
  649.1 331.8 all-reduce.2
  983.0 133.6 all-gather.5
where the time goes:
time: 1140 us
  waiting for transfers between devices  689 us (60%)
  matrix products  212 us (19%)
  blocking collectives  118 us (10%)
  local copies, waits for them, and re-layouts  51.4 us (5%)
  other arithmetic  30.2 us (3%)
  starting transfers between devices  20.7 us (2%)
  between operations  14.9 us (1%)
    psum x1, waiting for transfers between devices, shards(): lax.psum(summed[3].astype(jnp.bfloat16), 'seq').astype(jnp.float32)  223 us
    all_gather x1, waiting for transfers between devices, shards(): lax.all_gather(weights, 'wsh', axis=0, tiled=True)  160 us
    reduce_scatter x1, waiting for transfers between devices, shards(): lax.psum_scatter(g_gu.astype(jnp.bfloat16), 'wsh', scatter_dimension=0, t...  140 us
    reduce_scatter x1, waiting for transfers between devices, shards(): lax.psum_scatter(g_down.astype(jnp.bfloat16), 'wsh', scatter_dimension=0,...  81 us
    all_to_all x1, blocking collectives, shards(): lax.all_to_all(leaving[0], 'seq', split_axis=0, concat_axis=0, tiled=True)  58.2 us
    psum x1, blocking collectives, shards(): lax.psum(summed[4].astype(jnp.bfloat16), 'seq').astype(jnp.float32)  49.4 us
    dot_general x4, matrix products, contract_cols(): lax.dot_general(left, right, (((1,), (1,)), ((), ())), preferred_element_...  39.1 us
    dot_general x4, matrix products, contract_rows(): lax.dot_general(left, right, (((0,), (0,)), ((), ())), preferred_element_...  36 us
  transfers between devices with their start and end apart: 13, of which 10 were waited for; matrix products, arithmetic and copies ran while one was open for 18% of the time, Pallas kernels for 0%

commit v1 on v0

--- a/solution.py
+++ b/solution.py
@@ -12,6 +12,19 @@
 LEARN = 0.03
 LEARN_VEC = 0.05
 HIGH = lax.Precision.HIGHEST
+
+
+def replace_the_boxes(field_in, axis_tag):
+    n_shards = lax.axis_size(axis_tag)
+    block_list = tuple(((no, (no + 1) % n_shards) for no in range(n_shards)))
+    r2, shaped = ([field_in], [field_in])
+    gallery = tuple(((no, (no - 1) % n_shards) for no in range(n_shards)))
+    for _ in range(n_shards // 2):
+        r2.append(lax.ppermute(r2[-1], axis_tag, block_list))
+    for _ in range((n_shards - 1) // 2):
+        shaped.append(lax.ppermute(shaped[-1], axis_tag, gallery))
+    d_next = jnp.concatenate([*r2[::-1], *shaped[1:]], axis=0)
+    return jnp.roll(d_next, (lax.axis_index(axis_tag) - n_shards // 2) * field_in.shape[0], 0)
 
 
 def passed_along(block, axis, distance):
@@ -79,7 +92,7 @@
     x_bf = jnp.take(arrived[0], deal_order, axis=0).reshape(rows, D)
     dy_bf = jnp.take(arrived[1], deal_order, axis=0).reshape(rows, D)
     full_w, gains_bf, kernel_bf = (
-        lax.all_gather(weights, "wsh", axis=0, tiled=True),
+        replace_the_boxes(weights, "wsh"),
         lax.all_gather(norm_gains, "wsh", axis=1, tiled=True),
         lax.all_gather(conv_kernel, "wsh", axis=1, tiled=True),
     )

time: 1140 us -> 1290 us (1.13)
  blocking collectives: 118 us -> 276 us
  waiting for transfers between devices: 689 us -> 619 us
  local copies, waits for them, and re-layouts: 51.4 us -> 113 us
    all_gather x1 -> x0, waiting for transfers between devices: 160 us -> none  [shards(): lax.all_gather(weights, 'wsh', axis=0, tiled=True)]
    all_gather x1, blocking collectives: 5.21 us -> 162 us  [shards(): lax.all_gather(norm_gains, 'wsh', axis=1, tiled=True)]
    ppermute x0 -> x3, waiting for transfers between devices: none -> 102 us  [the longest x2 102 us: replace_the_boxes(): r2.append(lax.ppermute(r2[-1], axis_tag, block_list))]
    unnamed x60 -> x75, local copies, waits for them, and re-layouts: 8.24 us -> 63.1 us
    all_to_all x1, waiting for transfers between devices: 13.6 us -> 0.01 us  [shards(): lax.all_to_all(out_grad.reshape(n_seq, unit, D), 'seq', split_axis=0, con...]
  transfers between devices with their start and end apart: 13 -> 15, of which waited for: 10 -> 10; matrix products, arithmetic and copies ran while one was open for 18% -> 18% of each run, Pallas kernels for 0% -> 0%
where the time goes in v1:
time: 1290 us
  waiting for transfers between devices  619 us (48%)
  blocking collectives  276 us (21%)
  matrix products  211 us (16%)
  local copies, waits for them, and re-layouts  113 us (9%)
  other arithmetic  28.1 us (2%)
  starting transfers between devices  22.6 us (2%)
  between operations  15.1 us (1%)
    psum x1, waiting for transfers between devices, shards(): lax.psum(summed[3].astype(jnp.bfloat16), 'seq').astype(jnp.float32)  223 us
    all_gather x1, blocking collectives, shards(): lax.all_gather(norm_gains, 'wsh', axis=1, tiled=True)  162 us
    reduce_scatter x1, waiting for transfers between devices, shards(): lax.psum_scatter(g_gu.astype(jnp.bfloat16), 'wsh', scatter_dimension=0, t...  140 us
    ppermute x2, waiting for transfers between devices, replace_the_boxes(): r2.append(lax.ppermute(r2[-1], axis_tag, block_list))  102 us
    reduce_scatter x1, waiting for transfers between devices, shards(): lax.psum_scatter(g_down.astype(jnp.bfloat16), 'wsh', scatter_dimension=0,...  81.1 us
    unnamed x75, local copies, waits for them, and re-layouts  63.1 us
    all_to_all x1, blocking collectives, shards(): lax.all_to_all(leaving[0], 'seq', split_axis=0, concat_axis=0, tiled=True)  58.3 us
    psum x1, blocking collectives, shards(): lax.psum(summed[4].astype(jnp.bfloat16), 'seq').astype(jnp.float32)  49.4 us
  transfers between devices with their start and end apart: 15, of which 10 were waited for; matrix products, arithmetic and copies ran while one was open for 18% of the time, Pallas kernels for 0%

profile of v1, /device:TPU:0, one launch (start us, length us, event | category | flops | bytes accessed | tf_op | source)
XLA Modules:
  0.0 1285.1 jit_solution(11995519392868290568)
XLA Ops:
  7.7 101.8 %collective-permute-done = bf16[256,17920]{1,0:T(8,128)(2,1)} collective-permute-done((bf16[256,17920]{1,0:T(8,128)(2,1)}, bf16[256,17920]{1,0:T(8,128)(2,1)}, u32[]{:S(2)}, u32[]{:S(2)}) %collective-permute-start) | collective-permute-done | bytes 9175072 | tf_op jit(solution)/shard_map/ppermute | solution.py:23
  119.1 24.3 %all-to-all-done = bf16[8,64,1024]{2,1,0:T(8,128)(2,1)S(1)} async-done(((bf16[8,64,1024]{2,1,0:T(8,128)(2,1)}), bf16[8,64,1024]{2,1,0:T(8,128)(2,1)S(1)}, u32[]{:S(2)}, u32[]{:S(2)}) %all-to-all-start) | async-done | bytes 1048608 | tf_op jit(solution)/shard_map/all_to_all | solution.py:85
  147.8 162.4 %all_gather.9 = bf16[2,1024]{1,0:T(2,128)(2,1)S(1)} all-gather(bf16[2,256]{1,0:T(2,128)(2,1)S(1)} %copy-done.26), channel_id=1, replica_groups=mesh['seq'=8,'wsh'=4] {'wsh'}, dimensions={1}, use_global_device_ids=true | all-gather | bytes 5120 | tf_op jit(solution)/shard_map/all_gather | solution.py:96
  398.4 18.3 %fusion.4 = f32[512,9216]{1,0:T(8,128)} fusion(bf16[2048,17920]{1,0:T(8,128)(2,1)} %constant_dynamic-update-slice_fusion, s32[]{:T(128)S(6)} %select_n.29, s32[]{:T(128)S(6)} %add.141, f32[512,1024]{1,0:T(8,128)S(1)} %get-tuple-element.51, f32[1024]{0:T(1024)S(1)} %bitcast.101, f32[512]{0:T(512)S(1)} %add_rsqrt_fusion.1), kind=kOutput, calls=%fused_computation.10 | convolution fusion | flops 9665249280 | bytes 39852040 | tf_op jit(solution)/shard_map/dot_general | solution.py:123
  416.6 16.8 %multiply_convert_fusion.1 = (bf16[512,4608]{1,0:T(8,128)(2,1)}, bf16[512,4608]{1,0:T(8,128)(2,1)}, bf16[512,4608]{1,0:T(8,128)(2,1)}) fusion(f32[512,9216]{1,0:T(8,128)} %fusion.4, bf16[512,1024]{1,0:T(8,128)(2,1)S(1)} %bitcast.86, bf16[2048,17920]{1,0:T(8,128)(2,1)} %constant_dynamic-update-slice_fusion, s32[]{:T(128)S(6)} %select_n.29, s32[]{:T(128)S(6)} %add.142), kind=kOutput, calls=%fused_computation.15 | convolution fusion | flops 4869586944 | bytes 43515912 | tf_op jit(solution)/shard_map/dot_general | solution.py:131
  433.4 15.9 %multiply_reduce_fusion.1 = (bf16[1024]{0:T(1024)(128)(2,1)S(1)}, f32[512]{0:T(512)S(1)}, f32[512,1024]{1,0:T(8,128)S(1)}) fusion(f32[512,1024]{1,0:T(8,128)} %copy-done.10, f32[512]{0:T(512)S(1)} %add_rsqrt_fusion.1, f32[1024]{0:T(1024)S(1)} %bitcast.102, bf16[2048,17920]{1,0:T(8,128)(2,1)} %constant_dynamic-update-slice_fusion, s32[]{:T(128)S(6)} %select_n.29, ...), kind=kOutput, calls=%fused_computation.75 | convolution fusion | flops 9685694464 | bytes 32516104 | tf_op jit(solution)/shard_map/dot_general | solution.py:63
  477.1 9.8 convolution_convert_fusion.1
  488.5 17.3 %convolution_convert_fusion = bf16[1024,9216]{1,0:T(8,128)(2,1)} fusion(bf16[512,4608]{1,0:T(8,128)(2,1)} %get-tuple-element.32, bf16[512,4608]{1,0:T(8,128)(2,1)} %get-tuple-element.31, f32[512,1024]{1,0:T(8,128)S(1)} %copy-done.12, f32[1024]{0:T(1024)S(1)} %bitcast.104, f32[512]{0:T(512)S(1)} %add_rsqrt_fusion.1), kind=kOutput, calls=%fused_computation.7 | convolution fusion | flops 9693560832 | bytes 30414848 | tf_op jit(solution)/shard_map/dot_general | solution.py:57
  506.5 8.8 fusion.41
  516.1 32.7 %reduce-scatter.6.cloned.1.call-done = bf16[256,3072]{1,0:T(8,128)(2,1)} async-done(((bf16[1024,3072]{1,0:T(8,128)(2,1)}), bf16[256,3072]{1,0:T(8,128)(2,1)}) %reduce-scatter.6.cloned.1.call-update) | async-done | bytes 1572880 | tf_op jit(solution)/shard_map/reduce_scatter | solution.py:169
  548.8 81.1 %reduce-scatter.12.cloned.1.call-done = bf16[256,4608]{1,0:T(8,128)(2,1)} async-done(((bf16[1024,4608]{1,0:T(8,128)(2,1)}), bf16[256,4608]{1,0:T(8,128)(2,1)}) %reduce-scatter.12.cloned.1.call-update) | async-done | bytes 2359312 | tf_op jit(solution)/shard_map/reduce_scatter | solution.py:178
  630.0 140.3 %reduce-scatter.10.cloned.1.call-done = bf16[256,9216]{1,0:T(8,128)(2,1)} async-done(((bf16[1024,9216]{1,0:T(8,128)(2,1)}), bf16[256,9216]{1,0:T(8,128)(2,1)}) %reduce-scatter.10.cloned.1.call-update) | async-done | bytes 4718608 | tf_op jit(solution)/shard_map/reduce_scatter | solution.py:175
  774.2 9.9 add_convert_fusion
  793.5 58.3 %all_to_all.20 = bf16[8,64,1024]{2,1,0:T(8,128)(2,1)S(1)} all-to-all(bf16[8,64,1024]{2,1,0:T(8,128)(2,1)S(1)} %get-tuple-element.49), channel_id=1, replica_groups=mesh['seq'=8,'wsh'=4] {'seq'}, dimensions={0} | all-to-all | bytes 2097152 | tf_op jit(solution)/shard_map/all_to_all | solution.py:165
  855.5 49.4 %psum.39 = bf16[5,256]{1,0:T(8,128)(2,1)S(1)} all-reduce(bf16[5,256]{1,0:T(8,128)(2,1)} %reduce-scatter.14.cloned.1.call-done), channel_id=1, replica_groups=mesh['seq'=8,'wsh'=4] {'seq'}, use_global_device_ids=true, to_apply=%region_21.23 | all-reduce | flops 1280 | bytes 5120 | tf_op jit(solution)/shard_map/psum | solution.py:190
  906.4 222.6 %all-reduce.3.cloned.1.call-done = (bf16[256,4608]{1,0:T(8,128)(2,1)}, bf16[256,9216]{1,0:T(8,128)(2,1)}, bf16[256,1024]{1,0:T(8,128)(2,1)}, bf16[256,3072]{1,0:T(8,128)(2,1)}) async-done(((bf16[256,4608]{1,0:T(8,128)(2,1)}, bf16[256,9216]{1,0:T(8,128)(2,1)}, bf16[256,1024]{1,0:T(8,128)(2,1)}, bf16[256,3072]{1,0:T(8,128)(2,1)}), (bf16[256,4608]{1,0:T(8,128)(2,1)}, bf16[256,9216]{1,0:T(8,128)(2,1)}, ...) | async-done | bytes 9175056 | tf_op jit(solution)/shard_map/psum | solution.py:189
  1129.0 10.2 convert_multiply_fusion
  1139.2 19.2 %mul.437 = f32[2,128,140,128]{3,2,1,0:T(8,128)} reshape(f32[256,17920]{1,0:T(8,128)} %convert_multiply_fusion) | data formatting | bytes 36700160 | tf_op jit(solution)/shard_map/mul | solution.py:193
  1158.3 12.0 copy.22
  1170.4 29.5 %fusion.19 = f32[1,280,16,128]{3,2,1,0:T(8,128)S(1)} fusion(f32[2,280,16,128]{3,2,1,0:T(8,128)S(1)} %bitcast.83, f32[280,128,128]{2,1,0:T(8,128)S(1)} %bitcast.76, s32[]{:T(128)S(6)} %select_n.31), kind=kOutput, calls=%fused_computation.39 | convolution fusion | flops 882524160 | bytes 25231364 | tf_op jit(solution)/shard_map/nij,nkj->nik/dot_general | solution.py:208
  1199.9 35.2 %fusion.18 = f32[1,280,16,128]{3,2,1,0:T(8,128)S(1)} fusion(f32[2,280,16,128]{3,2,1,0:T(8,128)S(1)} %bitcast.83, f32[280,128,128]{2,1,0:T(8,128)S(1)} %bitcast.77, s32[]{:T(128)S(6)} %select_n.31), kind=kOutput, calls=%fused_computation.37 | convolution fusion | flops 882524160 | bytes 41287684 | tf_op jit(solution)/shard_map/nji,njk->nik/dot_general | solution.py:209
  1237.5 17.0 %fusion.16 = f32[280,128,16]{1,2,0:T(8,128)S(1)} fusion(f32[280,128,128]{2,1,0:T(8,128)S(1)} %bitcast.78, f32[2,280,16,128]{3,2,1,0:T(8,128)} %param.21), kind=kOutput, calls=%fused_computation.34 | convolution fusion | flops 880803840 | bytes 22937600 | tf_op jit(solution)/shard_map/nij,njk->nik/dot_general | solution.py:219
  1254.5 10.2 all-gather.3.cloned.1.call-done
  1264.7 10.6 fusion.52
  (163 shorter events, 156.5 us)
Async XLA Ops:
  7.2 140.6 %copy-start.26 = (bf16[2,256]{1,0:T(2,128)(2,1)S(1)}, bf16[2,256]{1,0:T(2,128)(2,1)}, u32[]{:S(2)}) copy-start(bf16[2,256]{1,0:T(2,128)(2,1)} %param.17) | copy-start | bytes 3076
  7.2 303.1 %copy-start.25 = (bf16[3,256]{1,0:T(4,128)(2,1)S(1)}, bf16[3,256]{1,0:T(4,128)(2,1)}, u32[]{:S(2)}) copy-start(bf16[3,256]{1,0:T(4,128)(2,1)} %param.18) | copy-start | bytes 4612
  7.2 308.8 %copy-start.27 = (s32[8]{0:T(128)S(1)}, s32[8]{0:T(128)}, u32[]{:S(2)}) copy-start(s32[8]{0:T(128)} %param.14) | copy-start | bytes 100
  7.2 102.4 %collective-permute-start = (bf16[256,17920]{1,0:T(8,128)(2,1)}, bf16[256,17920]{1,0:T(8,128)(2,1)}, u32[]{:S(2)}, u32[]{:S(2)}) collective-permute-start(bf16[256,17920]{1,0:T(8,128)(2,1)} %param.16), channel_id=1, source_target_pairs={{0,1},{1,2},{2,3},{3,0},{4,5},{5,6},{6,7},{7,4},{8,9},{9,10},{10,1... | collective-permute-start | bytes 27525128 | tf_op jit(solution)/shard_map/ppermute | solution.py:23
  109.6 209.9 %collective-permute-start.1 = (bf16[256,17920]{1,0:T(8,128)(2,1)}, bf16[256,17920]{1,0:T(8,128)(2,1)}, u32[]{:S(2)}, u32[]{:S(2)}) collective-permute-start(bf16[256,17920]{1,0:T(8,128)(2,1)} %collective-permute-done), channel_id=1, source_target_pairs={{0,1},{1,2},{2,3},{3,0},{4,5},{5,6},{6,7},{7,4},{8,9},{9,10},{10,1... | collective-permute-start | bytes 27525128 | tf_op jit(solution)/shard_map/ppermute | solution.py:23
  109.6 33.8 %all-to-all-start = ((bf16[8,64,1024]{2,1,0:T(8,128)(2,1)}), bf16[8,64,1024]{2,1,0:T(8,128)(2,1)S(1)}, u32[]{:S(2)}, u32[]{:S(2)}) async-start(bf16[8,64,1024]{2,1,0:T(8,128)(2,1)} %bitcast.90), calls=%async_computation | async-start | bytes 2097152 | tf_op jit(solution)/shard_map/all_to_all | solution.py:85
  116.2 227.0 %collective-permute-start.2 = (bf16[256,17920]{1,0:T(8,128)(2,1)}, bf16[256,17920]{1,0:T(8,128)(2,1)}, u32[]{:S(2)}, u32[]{:S(2)}) collective-permute-start(bf16[256,17920]{1,0:T(8,128)(2,1)} %param.16), channel_id=1, source_target_pairs={{0,3},{1,0},{2,1},{3,2},{4,7},{5,4},{6,5},{7,6},{8,11},{9,8},{10,9... | collective-permute-start | bytes 27525128 | tf_op jit(solution)/shard_map/ppermute | solution.py:25
  143.4 173.9 %all-to-all-start.2 = ((bf16[8,64,1024]{2,1,0:T(8,128)(2,1)}), bf16[8,64,1024]{2,1,0:T(8,128)(2,1)}, u32[]{:S(2)}, u32[]{:S(2)}) async-start(bf16[8,64,1024]{2,1,0:T(8,128)(2,1)} %bitcast.91), calls=%async_computation.2 | async-start | bytes 2097152 | tf_op jit(solution)/shard_map/all_to_all | solution.py:88
  147.6 368.5 %reduce-scatter.8.cloned.1.call-start = ((), (), s32[]{:S(2)}) async-start(), calls=%async_computation.10 | async-start | bytes 2621440 | tf_op jit(solution)/shard_map/reduce_scatter | solution.py:172
  319.4 62.3 %copy-start.18 = (bf16[512,1024]{1,0:T(8,128)(2,1)}, bf16[512,1024]{1,0:T(8,128)(2,1)S(1)}, u32[]{:S(2)}) copy-start(bf16[512,1024]{1,0:T(8,128)(2,1)S(1)} %fusion.32) | copy-start | bytes 3145732
  387.7 4.9 collective-permute-start.3
  391.9 57.4 %copy-start.8 = (bf16[8,64,1024]{2,1,0:T(8,128)(2,1)}, bf16[8,64,1024]{2,1,0:T(8,128)(2,1)S(1)}, u32[]{:S(2)}) copy-start(bf16[8,64,1024]{2,1,0:T(8,128)(2,1)S(1)} %broadcast_select_fusion.2) | copy-start | bytes 3145732
  398.3 18.3 %copy-start.10 = (f32[512,1024]{1,0:T(8,128)}, f32[512,1024]{1,0:T(8,128)S(1)}, u32[]{:S(2)}) copy-start(f32[512,1024]{1,0:T(8,128)S(1)} %get-tuple-element.51) | copy-start | bytes 6291460
  454.0 94.8 %reduce-scatter.6.cloned.1.call-start = ((), (), s32[]{:S(2)}) async-start(), calls=%async_computation.9 | async-start | bytes 7864320 | tf_op jit(solution)/shard_map/reduce_scatter | solution.py:169
  459.1 6.1 collective-permute-start.4
  475.9 154.1 %reduce-scatter.12.cloned.1.call-start = ((), (), s32[]{:S(2)}) async-start(), calls=%async_computation.12 | async-start | bytes 11796480 | tf_op jit(solution)/shard_map/reduce_scatter | solution.py:178
  486.9 283.3 %reduce-scatter.10.cloned.1.call-start = ((), (), s32[]{:S(2)}) async-start(), calls=%async_computation.11 | async-start | bytes 23592960 | tf_op jit(solution)/shard_map/reduce_scatter | solution.py:175
  505.9 349.6 %reduce-scatter.14.cloned.1.call-start = ((), (), s32[]{:S(2)}) async-start(), calls=%async_computation.13 | async-start | bytes 20480 | tf_op jit(solution)/shard_map/reduce_scatter | solution.py:181
  516.0 612.9 %all-reduce.3.cloned.1.call-start = ((), (), s32[]{:S(2)}) async-start(), calls=%async_computation.15 | async-start | bytes 18350080 | tf_op jit(solution)/shard_map/psum | solution.py:189
  770.3 494.4 %all-gather.3.cloned.1.call-start = ((), (), s32[]{:S(2)}) async-start(), calls=%async_computation.14 | async-start | bytes 10321920 | tf_op jit(solution)/shard_map/all_gather | solution.py:216
  793.4 111.4 %copy-start.24 = (f32[5,256]{1,0:T(8,128)S(1)}, f32[5,256]{1,0:T(8,128)}, u32[]{:S(2)}) copy-start(f32[5,256]{1,0:T(8,128)} %param.19) | copy-start | bytes 15364
  851.7 54.6 %all-to-all-start.3 = ((bf16[8,64,1024]{2,1,0:T(8,128)(2,1)}), bf16[8,64,1024]{2,1,0:T(8,128)(2,1)S(1)}, u32[]{:S(2)}, u32[]{:S(2)}) async-start(bf16[8,64,1024]{2,1,0:T(8,128)(2,1)} %get-tuple-element.48), calls=%async_computation.3 | async-start | bytes 2097152 | tf_op jit(solution)/shard_map/all_to_all | solution.py:166
  906.4 222.6 %copy-start.6 = (bf16[8,64,1024]{2,1,0:T(8,128)(2,1)}, bf16[8,64,1024]{2,1,0:T(8,128)(2,1)S(1)}, u32[]{:S(2)}) copy-start(bf16[8,64,1024]{2,1,0:T(8,128)(2,1)S(1)} %all-to-all-done.3) | copy-start | bytes 3145732
  1139.2 31.2 %slice-start.2 = ((s8[4587520]{0:T(1024)(128)(4,1)}), s8[393216]{0:T(1024)(128)(4,1)S(1)}, s32[]{:S(2)}) async-start(s8[4587520]{0:T(1024)(128)(4,1)} %bitcast.82), calls=%async_computation.18 | async-start | bytes 786432
  (24 other events, 119.9 us)
Sparse Core Ops, SparseCore 0:
  454.2 33.2 reduce-scatter.7
  489.9 58.8 reduce-scatter.5
  552.0 77.9 reduce-scatter.11
  632.4 137.8 reduce-scatter.9
  773.1 19.5 reduce-scatter.13
  797.0 331.8 all-reduce.2
  1131.0 133.6 all-gather.2
